TPU v7x, 32 devices: a whole 2x2x4 slice. The times are simulated.
32 devices in a mesh: curve: 8 (over z, x), head: 4 (over y, core).
Axes of the slice: x: 2, y: 2, z: 4, core: 2. Of those that a mesh axis runs over, the one named last changes fastest.
Arguments:
- points: bfloat16 [16384, 1024], P(('curve', 'head')), may hold values from -6 to 6
- order: int32 [32, 512], P(('curve', 'head')), may hold values from 0 to 511, each once within a row
- scan_ids: int32 [16384], P(('curve', 'head')), may hold values from 0 to 3
- ln_gain: float32 [2, 1024], replicated, may hold values from 0.25 to 1.75
- w_qkv: bfloat16 [2, 1024, 3072], P(None, None, 'head'), may hold values from -7 to 7, as said below
- w_out: bfloat16 [2, 1024, 1024], P(None, 'head'), may hold values from -0.1875 to 0.1875
Outputs:
- refined: bfloat16 [16384, 1024], P(('curve', 'head'))
Inputs may be any that keep to these rules, and one draw needn't show every extreme that they name: `order`: row b is a permutation of the 512 rows of block b. `w_qkv`: columns ordered by head, then query, key, value, then entry.
All inputs are finite; a program needn't handle non-finite values.
Results may differ from a plain program's by a relative error of at most 0.01.
Values may be sent and summed in bfloat16 or wider, within the bound.
A program may use at most 64 MiB of HBM per device.

v0:
```python
import functools

import jax
import jax.numpy as jnp
from jax import lax
from jax.experimental import pallas as pl
from jax.experimental.pallas import tpu as pltpu
from jax.sharding import PartitionSpec as P

HEAD_DIM = 64
PATCH = 1024


EPSILON = 1e-05


def layer_norm(rows, gain):
    values = rows.astype(jnp.float32)
    center = values - jnp.mean(values, axis=-1, keepdims=True)
    spread = jnp.mean(center * center, axis=-1, keepdims=True)
    return (center * lax.rsqrt(spread + EPSILON) * gain).astype(jnp.bfloat16)


def remote(src, dst, send_sem, recv_sem, device):
    return pltpu.make_async_remote_copy(
        src_ref=src,
        dst_ref=dst,
        send_sem=send_sem,
        recv_sem=recv_sem,
        device_id=device,
        device_id_type=pl.DeviceIdType.MESH,
    )


def layer_kernel(
    peers, ranges, halo, x_ref, tag_ref, w_ref, wo_ref, stream_ref, out_ref,
    all_x, q_buf, kv_buf, tags, att, heads, all_wo,
    x_recv, x_send, w_recv, w_send, t_recv, t_send, h_recv, h_send, kv_recv, kv_send,
):
    chunks, chunk_rows, _ = x_ref.shape
    rows = chunks * chunk_rows
    heads_local = w_ref.shape[1] // (3 * HEAD_DIM)
    chips = peers // 2
    window_blocks = PATCH // rows
    curve = lax.axis_index("curve")
    me = lax.axis_index("head")
    chip, core = me // 2, me % 2
    partner = chip * 2 + 1 - core
    up, down = {"curve": (curve + 1) % ranges}, {"curve": (curve + ranges - 1) % ranges}
    same = [((chip + s) % chips) * 2 + core for s in range(chips)]
    other = [((chip + s) % chips) * 2 + 1 - core for s in range(chips)]
    others = [(me + t) % peers for t in range(1, peers)]

    barrier = pltpu.get_barrier_semaphore()
    for blk in others:
        pl.semaphore_signal(
            barrier, inc=1, device_id={"head": blk}, device_id_type=pl.DeviceIdType.MESH
        )
    if halo:
        for neighbour in (up, down):
            pl.semaphore_signal(
                barrier, inc=1, device_id=neighbour, device_id_type=pl.DeviceIdType.MESH
            )
    pl.semaphore_wait(barrier, peers - 1 + (2 if halo else 0))

    def direct_x(s, c):
        dest = partner if s == 0 else same[s]
        return remote(
            x_ref.at[c], all_x.at[me, c], x_send.at[s, c], x_recv.at[me, c], {"head": dest}
        )

    def passed_x(s, c):
        part = all_x.at[same[s], c]
        return remote(
            part, part, x_send.at[chips + s, c], x_recv.at[same[s], c], {"head": partner}
        )

    def wait_x(blk, c):
        part = all_x.at[blk, c]
        remote(part, part, x_send.at[0, c], x_recv.at[blk, c], {"head": partner}).wait_recv()

    def tag_copy(t):
        return remote(
            tag_ref.at[0], tags.at[halo + me], t_send.at[t], t_recv.at[halo + me],
            {"head": others[t]},
        )

    def direct_w(s):
        dest = partner if s == 0 else same[s]
        return remote(wo_ref, all_wo.at[me], w_send.at[s], w_recv.at[me], {"head": dest})

    def passed_w(s):
        part = all_wo.at[same[s]]
        return remote(
            part, part, w_send.at[chips + s], w_recv.at[same[s]], {"head": partner}
        )

    def wait_w(blk):
        part = all_wo.at[blk]
        remote(part, part, w_send.at[0], w_recv.at[blk], {"head": partner}).wait_recv()

    def edge(buffer, send, recv, j):
        if j < halo:
            src, dst, device = buffer.at[peers + j], buffer.at[j], up
        else:
            src, dst, device = buffer.at[j], buffer.at[peers + j], down
        return remote(src, dst, send.at[j], recv.at[j], device)

    tag_send_edge = peers - 1

    for s in range(chips):
        for c in range(chunks):
            direct_x(s, c).start()
    for t in range(peers - 1):
        tag_copy(t).start()
    direct_w(0).start()
    tags[halo + me] = tag_ref[0]

    def project(values, blk, first_row):
        result = jnp.dot(values, w_ref[...], preferred_element_type=jnp.float32)
        result = result.astype(jnp.bfloat16)
        at = pl.ds(first_row, chunk_rows)
        for head in range(heads_local):
            base = head * 3 * HEAD_DIM
            q_buf[blk, at, head * HEAD_DIM : (head + 1) * HEAD_DIM] = result[
                :, base : base + HEAD_DIM
            ] * jnp.bfloat16(HEAD_DIM ** (-0.5))
            kv_buf[halo + blk, at, head * 2 * HEAD_DIM : (head + 1) * 2 * HEAD_DIM] = result[
                :, base + HEAD_DIM : base + 3 * HEAD_DIM
            ]

    def project_block(blk):
        for c in range(chunks):
            project(all_x[blk, c], blk, c * chunk_rows)

    def attend(blk):
        first = (blk + halo) // window_blocks * window_blocks
        column = jnp.transpose(
            jnp.broadcast_to(tags[halo + blk].astype(jnp.float32), (128, rows))
        )[:, :1]
        line = jnp.concatenate(
            [tags[first + j].astype(jnp.float32) for j in range(window_blocks)], axis=1
        )
        bias = jnp.where(column == line, 0.0, -jnp.inf)
        ones = jnp.ones((PATCH, HEAD_DIM), jnp.bfloat16)
        for head in range(heads_local):
            at = head * 2 * HEAD_DIM
            wide = kv_buf[pl.ds(first, window_blocks), :, at : at + 2 * HEAD_DIM].reshape(
                PATCH, 2 * HEAD_DIM
            )
            query = q_buf[blk, :, head * HEAD_DIM : (head + 1) * HEAD_DIM]
            scores = lax.dot_general(
                query, wide[:, :HEAD_DIM], (((1,), (1,)), ((), ())),
                preferred_element_type=jnp.float32,
            ) + bias
            row_max = jnp.max(scores, axis=-1, keepdims=True)
            expo = jnp.exp(scores - row_max).astype(jnp.bfloat16)
            result = jnp.dot(
                expo,
                jnp.concatenate([wide[:, HEAD_DIM:], ones], axis=1),
                preferred_element_type=jnp.float32,
            )
            normal = result[:, :HEAD_DIM] / result[:, HEAD_DIM : HEAD_DIM + 1]
            att[blk, :, head * HEAD_DIM : (head + 1) * HEAD_DIM] = normal.astype(jnp.bfloat16)

    def head_copy(t):
        blk = others[t]
        return remote(
            att.at[blk], heads.at[me], h_send.at[t], h_recv.at[me], {"head": blk}
        )

    def head_copy_to(blk):
        t = (blk - me + peers - 1) % peers
        return remote(
            att.at[blk], heads.at[me], h_send.at[t], h_recv.at[me], {"head": blk}
        )

    for c in range(chunks):
        project(x_ref[c], me, c * chunk_rows)
    for c in range(chunks):
        wait_x(partner, c)
    project_block(partner)
    for blk in others:
        part = tags.at[halo + blk]
        remote(part, part, t_send.at[0], t_recv.at[halo + blk], {"head": partner}).wait_recv()
    if halo:
        for j in range(2 * halo):
            edge(tags, t_send.at[pl.ds(peers, 2 * halo)], t_recv.at[pl.ds(peers + 2 * halo, 2 * halo)], j).start()

    early = not halo and window_blocks == 2
    if early:
        attend(me)
        attend(partner)
        head_copy_to(partner).start()
    for s in range(1, chips):
        for c in range(chunks):
            wait_x(same[s], c)
            passed_x(s, c).start()
            project(all_x[same[s], c], same[s], c * chunk_rows)
    for s in range(1, chips):
        direct_w(s).start()
        for c in range(chunks):
            wait_x(other[s], c)
            project(all_x[other[s], c], other[s], c * chunk_rows)
    if halo:
        for j in range(2 * halo):
            edge(kv_buf, kv_send, kv_recv, j).start()
        middle = chips // 2 if window_blocks == 2 else 0
        for j in range(2 * halo):
            edge(tags, t_send.at[pl.ds(peers, 2 * halo)], t_recv.at[pl.ds(peers + 2 * halo, 2 * halo)], j).wait_recv()

    def finish(blk):
        attend(blk)

        @pl.when(blk != me)
        def _():
            head_copy_to(blk).start()

    if early:
        for s in range(1, chips):
            finish(other[s])
            finish(same[s])
    else:
        if halo:
            inner = list(range(halo, peers - halo))
            outer = list(range(peers - halo, peers)) + list(range(halo))

            def inner_step(i, carry):
                finish(halo + (me + 1 + i) % (peers - 2 * halo))
                return carry

            lax.fori_loop(0, len(inner), inner_step, 0)
            for j in range(2 * halo):
                edge(kv_buf, kv_send, kv_recv, j).wait_recv()

            def outer_step(i, carry):
                finish((peers - halo + (me + i) % (2 * halo)) % peers)
                return carry

            lax.fori_loop(0, len(outer), outer_step, 0)
        else:

            def step(i, carry):
                finish((me + 1 + i) % peers)
                return carry

            lax.fori_loop(0, peers, step, 0)

    wait_w(partner)
    for s in range(1, chips):
        wait_w(same[s])
        passed_w(s).start()
    heads[me] = att[me]
    all_wo[me] = wo_ref[...]
    for s in range(1, chips):
        wait_w(other[s])
    for blk in others:
        part = heads.at[blk]
        remote(part, part, h_send.at[0], h_recv.at[blk], {"head": partner}).wait_recv()

    for c in range(chunks):
        at = pl.ds(c * chunk_rows, chunk_rows)
        total = stream_ref[at, :].astype(jnp.float32)
        for blk in range(peers):
            total += jnp.dot(
                heads[blk, at, :], all_wo[blk], preferred_element_type=jnp.float32
            )
        out_ref[at, :] = total.astype(jnp.bfloat16)

    for s in range(chips):
        for c in range(chunks):
            direct_x(s, c).wait_send()
            if s:
                passed_x(s, c).wait_send()
        direct_w(s).wait_send()
        if s:
            passed_w(s).wait_send()
    for t in range(peers - 1):
        tag_copy(t).wait_send()
        head_copy(t).wait_send()
    for j in range(2 * halo):
        edge(tags, t_send.at[pl.ds(peers, 2 * halo)], t_recv.at[pl.ds(peers + 2 * halo, 2 * halo)], j).wait_send()
        edge(kv_buf, kv_send, kv_recv, j).wait_send()


def layer(index, stream, normed, tag_row, weights, out_weights):
    rows, width = stream.shape
    peers, ranges = lax.axis_size("head"), lax.axis_size("curve")
    halo = PATCH // 2 // rows if index else 0
    chips = peers // 2
    chunks = max(1, rows // 256)
    columns = out_weights.shape[0]
    vmem = pl.BlockSpec(memory_space=pltpu.VMEM)
    dma = pltpu.SemaphoreType.DMA
    bf16 = jnp.bfloat16
    return pl.pallas_call(
        functools.partial(layer_kernel, peers, ranges, halo),
        out_shape=jax.ShapeDtypeStruct((rows, width), bf16),
        in_specs=[vmem] * 5,
        out_specs=vmem,
        scratch_shapes=[
            pltpu.VMEM((peers, chunks, rows // chunks, width), bf16),
            pltpu.VMEM((peers, rows, columns), bf16),
            pltpu.VMEM((peers + 2 * halo, rows, 2 * columns), bf16),
            pltpu.VMEM((peers + 2 * halo, 1, rows), jnp.int32),
            pltpu.VMEM((peers, rows, columns), bf16),
            pltpu.VMEM((peers, rows, columns), bf16),
            pltpu.VMEM((peers, columns, width), bf16),
            dma((peers, chunks)),
            dma((peers, chunks)),
            dma((peers,)),
            dma((peers,)),
            dma((peers + 4 * halo,)),
            dma((peers + 2 * halo,)),
            dma((peers,)),
            dma((peers,)),
            dma((max(1, 2 * halo),)),
            dma((max(1, 2 * halo),)),
        ],
        compiler_params=pltpu.CompilerParams(collective_id=index, has_side_effects=True),
        cost_estimate=pl.CostEstimate(
            flops=20 * rows * width * width, bytes_accessed=20 * rows * width, transcendentals=0
        ),
    )(
        normed.reshape(chunks, rows // chunks, width),
        tag_row,
        weights,
        out_weights,
        stream,
    )


def on_device(points, order, scan_ids, ln_gain, w_qkv, w_out):
    stream = points[order[0]]
    tag_row = scan_ids.reshape(1, 1, -1)
    for index in range(2):
        normed = layer_norm(stream, ln_gain[index])
        stream = layer(index, stream, normed, tag_row, w_qkv[index], w_out[index])
    return stream


def solution(mesh):
    in_specs = (
        P(("curve", "head"), None),
        P(("curve", "head"), None),
        P(("curve", "head")),
        P(),
        P(None, None, "head"),
        P(None, "head", None),
    )
    out_specs = P(("curve", "head"), None)
    return jax.shard_map(
        on_device, mesh=mesh, in_specs=in_specs, out_specs=out_specs, check_vma=False
    )
```

profile of v0, /device:TPU:0, one launch (start us, length us, event | category | flops | bytes accessed | tf_op | source)
XLA Modules:
  0.0 151.4 jit_solution(12509614390691637078)
XLA Ops:
  0.0 0.0 copy-start
  0.0 0.8 compare_select_fusion
  0.8 0.8 fusion.5
  1.6 0.0 copy-done
  1.6 2.1 %gather_fusion = bf16[512,1024]{1,0:T(8,128)(2,1)S(1)} fusion(bf16[512,1024]{1,0:T(8,128)(2,1)S(1)} %copy-done, s32[1024]{0:T(1024)S(1)} %pad_clamp_fusion), kind=kCustom, calls=%fused_computation | custom fusion | bytes 2099200 | tf_op jit(solution)/shard_map/gather | solution.py:334
  3.6 0.0 copy-start.1
  3.7 0.0 copy-start.4
  3.7 0.2 convert_reduce_fusion.1
  3.9 0.4 multiply_reduce_fusion
  4.3 0.0 copy-start.3
  4.4 1.4 multiply_convert_fusion.x_ref
  5.7 0.0 copy-done.1
  5.7 0.0 copy-done.4
  5.7 1.1 slice_bitcast_fusion.2
  6.8 0.0 copy-done.3
  6.8 1.9 %slice_bitcast_fusion = (bf16[1024,768]{1,0:T(8,128)(2,1)}, bf16[1024,768]{1,0:T(8,128)(2,1)}) fusion(bf16[2,1024,768]{2,1,0:T(8,128)(2,1)S(1)} %copy-done.3), kind=kLoop, calls=%fused_computation.10 | loop fusion | bytes 6291456 | tf_op jit(solution)/shard_map/squeeze | solution.py:338
  8.7 64.9 %shard_map.64.stream_ref = bf16[512,1024]{1,0:T(8,128)(2,1)} custom-call(bf16[2,256,1024]{2,1,0:T(8,128)(2,1)} %multiply_convert_fusion.x_ref, s32[1,1,512]{2,1,0:T(1,128)} %bitcast.22, bf16[1024,768]{1,0:T(8,128)(2,1)} %get-tuple-element.6.w_ref, bf16[256,1024]{1,0:T(8,128)(2,1)} %get-tuple-element.8.wo_ref, bf16[512,1024]{1,0:T(8,128)(2,1)} %copy-done.1), custom_call_target="tpu_custom_call" | custom-call | flops 10737418240 | bytes 10485760 | tf_op jit(solution)/shard_map/pallas_call | solution.py:296
  73.6 0.0 copy-start.2
  73.6 1.5 %convert_reduce_fusion = f32[512]{0:T(512)S(1)} fusion(bf16[512,1024]{1,0:T(8,128)(2,1)} %shard_map.64.stream_ref), kind=kLoop, calls=%fused_computation.2 | loop fusion | flops 1048064 | bytes 1050624 | tf_op jit(solution)/shard_map/reduce_sum | solution.py:19
  75.1 1.6 %fusion.2 = f32[512]{0:T(512)S(1)} fusion(bf16[512,1024]{1,0:T(8,128)(2,1)} %shard_map.64.stream_ref, f32[512]{0:T(512)S(1)} %broadcast_multiply_fusion), kind=kLoop, calls=%fused_computation.5 | loop fusion | flops 2096640 | bytes 1052672 | tf_op jit(solution)/shard_map/reduce_sum | solution.py:20
  76.8 0.0 copy-done.2
  76.8 1.4 fusion.4
  78.1 71.0 %shard_map.65 = bf16[512,1024]{1,0:T(8,128)(2,1)} custom-call(bf16[2,256,1024]{2,1,0:T(8,128)(2,1)} %bitcast.18, s32[1,1,512]{2,1,0:T(1,128)} %bitcast.23, bf16[1024,768]{1,0:T(8,128)(2,1)} %get-tuple-element.5.w_ref, bf16[256,1024]{1,0:T(8,128)(2,1)} %get-tuple-element.7.wo_ref, bf16[512,1024]{1,0:T(8,128)(2,1)} %shard_map.64.stream_ref), custom_call_target="tpu_custom_call" | custom-call | flops 10737418240 | bytes 10485760 | tf_op jit(solution)/shard_map/pallas_call | solution.py:296
  149.2 2.3 %copy.8 = bf16[512,1024]{1,0:T(8,128)(2,1)} copy(bf16[512,1024]{1,0:T(8,128)(2,1)} %shard_map.65) | data formatting | bytes 2097152
  (7 shorter events, 0.1 us)
Async XLA Ops:
  0.0 1.6 %copy-start = (bf16[512,1024]{1,0:T(8,128)(2,1)S(1)}, bf16[512,1024]{1,0:T(8,128)(2,1)}, u32[]{:S(2)}) copy-start(bf16[512,1024]{1,0:T(8,128)(2,1)} %param.6) | copy-start | bytes 3145732
  3.6 2.1 %copy-start.1 = (bf16[512,1024]{1,0:T(8,128)(2,1)}, bf16[512,1024]{1,0:T(8,128)(2,1)S(1)}, u32[]{:S(2)}) copy-start(bf16[512,1024]{1,0:T(8,128)(2,1)S(1)} %gather_fusion) | copy-start | bytes 3145732
  3.7 2.0 %copy-start.4 = (bf16[2,256,1024]{2,1,0:T(8,128)(2,1)S(1)}, bf16[2,256,1024]{2,1,0:T(8,128)(2,1)}, u32[]{:S(2)}) copy-start(bf16[2,256,1024]{2,1,0:T(8,128)(2,1)} %param.11) | copy-start | bytes 3145732
  4.3 2.5 %copy-start.3 = (bf16[2,1024,768]{2,1,0:T(8,128)(2,1)S(1)}, bf16[2,1024,768]{2,1,0:T(8,128)(2,1)}, u32[]{:S(2)}) copy-start(bf16[2,1024,768]{2,1,0:T(8,128)(2,1)} %param.10) | copy-start | bytes 9437188
  73.6 3.2 %copy-start.2 = (bf16[512,1024]{1,0:T(8,128)(2,1)S(1)}, bf16[512,1024]{1,0:T(8,128)(2,1)}, u32[]{:S(2)}) copy-start(bf16[512,1024]{1,0:T(8,128)(2,1)} %shard_map.64.stream_ref) | copy-start | bytes 3145732
where the time goes:
time: 152 us; the launch traced here: 151 us
  Pallas kernels  136 us (89%)
  local copies, waits for them, and re-layouts  8.11 us (5%)
  other arithmetic  7.3 us (5%)
    pallas_call x2, Pallas kernels, layer(): pl.pallas_call(functools.partial(layer_kernel, peers, ranges, halo), out_...  136 us

commit v1 on v0

--- a/solution.py
+++ b/solution.py
@@ -330,7 +330,423 @@
     )
 
 
+SCANS = 4
+BLOCKED = -1e30
+LOG2_SCALE = 1.4426950408889634 * HEAD_DIM ** (-0.5)
+LANES = 128
+
+
+def pieces(index, extent):
+    alone = extent // 8 if index == 0 else 0
+    return alone, (extent - 2 * alone) // 4
+
+
+def fused_kernel(
+    peers, ranges,
+    points_ref, order_ref, tag_ref, gain_ref, wq_hbm, wo_hbm, out_ref,
+    xs, stream, wq, wo, query, keys, values, att, acc, peak, tags, tag_q, tag_k,
+    send_sem, recv_sem, load_sem,
+):
+    rows, width = points_ref.shape
+    layers, steps, _, columns = wq.shape
+    depth = wo_hbm.shape[1]
+    curve = lax.axis_index("curve")
+    me = lax.axis_index("head")
+    chip, core = me // 2, me % 2
+    x_at, z_at = curve % 2, curve // 2 % 2
+    partner = {"head": chip * 2 + 1 - core}
+    across = {"head": (me + 2) % peers}
+    beside = {"curve": curve + 1 - 2 * x_at}
+    above = {"curve": curve + 2 - 4 * z_at}
+    total = peers * ranges
+    block = (curve * peers + me + 2 * core - 1 + total) % total
+    pair = {"curve": block // peers, "head": block % peers}
+
+    bf16, f32 = jnp.bfloat16, jnp.float32
+    lane = lax.broadcasted_iota(jnp.int32, (1, LANES), 1)
+    low = lane < HEAD_DIM
+    numbers, order_of_sends = {}, []
+
+    def number(key):
+        return numbers.setdefault(key, len(numbers))
+
+    def copy(key, src, dst, device):
+        at = number(key)
+        return remote(src, dst, send_sem.at[at], recv_sem.at[at], device)
+
+    def send(key, src, dst, device):
+        order_of_sends.append((key, src, dst, device))
+        copy(key, src, dst, device).start()
+
+    def arrive(key, part):
+        copy(key, part, part, partner).wait_recv()
+
+    barrier = pltpu.get_barrier_semaphore()
+    for device in (partner, across, beside, above, pair):
+        pl.semaphore_signal(
+            barrier, inc=1, device_id=device, device_id_type=pl.DeviceIdType.MESH
+        )
+
+    loads = []
+    for index in range(layers):
+        for p in range(2):
+            loads.append((wq_hbm.at[index, :, pl.ds(p * columns, columns)], wq.at[index, p]))
+        loads.append((wo_hbm.at[index], wo.at[index, 0]))
+
+    def load(n):
+        return pltpu.make_async_copy(loads[n][0], loads[n][1], load_sem.at[n])
+
+    for n in range(len(loads)):
+        load(n).start()
+
+    def home(index, chunk):
+        if chunk < 2:
+            return wq_hbm.at[index, :, pl.ds(chunk * columns, columns)], wq.at[index, 4 + 2 * chunk]
+        return wo_hbm.at[index], wo.at[index, 2]
+
+    def extent(chunk):
+        return width if chunk < 2 else depth
+
+    def cut(index, chunk, kind):
+        alone, shared = pieces(index, extent(chunk))
+        cuts = 2 if chunk < 2 else 1
+        size = alone if kind[0] == "a" else shared
+        if not size:
+            return []
+        x_of = x_at if kind[1] == "s" else 1 - x_at
+        if kind[0] == "a":
+            base = x_of * alone
+        else:
+            z_of = z_at if kind[2] == "s" else 1 - z_at
+            base = 2 * alone + (x_of * 2 + z_of) * shared
+        size //= cuts
+        return [pl.ds(pl.multiple_of(base + c * size, 16), size) for c in range(cuts)]
+
+    kinds = ("qss", "qso", "qos", "qoo", "as", "ao")
+    every = [(index, chunk) for index in range(layers) for chunk in range(3)]
+    homes = {which: home(*which) for which in every}
+    theres = {
+        (index, chunk): wq.at[index, 5 + 2 * chunk] if chunk < 2 else wo.at[index, 3]
+        for index, chunk in every
+    }
+    parts_of = {
+        (*which, kind): [homes[which][1].at[at] for at in cut(*which, kind)]
+        for which in every
+        for kind in kinds
+    }
+
+    def first(index, chunk):
+        source, _ = homes[index, chunk]
+        for kind in ("qss", "as"):
+            for c, at in enumerate(cut(index, chunk, kind)):
+                part = parts_of[index, chunk, kind][c]
+                send(("y", index, chunk, kind, c), source.at[at], part, across)
+
+    def second(index, chunk):
+        for c, part in enumerate(parts_of[index, chunk, "qss"]):
+            arrive(("y", index, chunk, "qss", c), part)
+            send(("x", index, chunk, "q", c), part, part, beside)
+            send(("z", index, chunk, "s", c), part, part, above)
+
+    def third(index, chunk):
+        for c, part in enumerate(parts_of[index, chunk, "as"]):
+            arrive(("y", index, chunk, "as", c), part)
+            send(("x", index, chunk, "a", c), part, part, beside)
+        for c, part in enumerate(parts_of[index, chunk, "qos"]):
+            arrive(("x", index, chunk, "q", c), part)
+            send(("z", index, chunk, "o", c), part, part, above)
+
+    def fourth(index, chunk):
+        for c, part in enumerate(parts_of[index, chunk, "ao"]):
+            arrive(("x", index, chunk, "a", c), part)
+        for c, part in enumerate(parts_of[index, chunk, "qso"]):
+            arrive(("z", index, chunk, "s", c), part)
+        for c, part in enumerate(parts_of[index, chunk, "qoo"]):
+            arrive(("z", index, chunk, "o", c), part)
+        send(("f", index, chunk), homes[index, chunk][1], theres[index, chunk], partner)
+
+    def fifth(index, chunk):
+        arrive(("f", index, chunk), theres[index, chunk])
+
+    def share(index, chunk):
+        source, _ = home(index, chunk)
+        there = wq.at[index, 2 + chunk] if chunk < 2 else wo.at[index, 1]
+        send(("w", index, chunk), source, there, partner)
+
+    def shared(index, chunk):
+        there = wq.at[index, 2 + chunk] if chunk < 2 else wo.at[index, 1]
+        arrive(("w", index, chunk), there)
+
+    def column_of(row):
+        return jnp.transpose(jnp.broadcast_to(row.astype(f32), (LANES, row.shape[1])))
+
+    def key_tags(slot):
+        spot = (lane % HEAD_DIM).astype(f32)
+        return jnp.where(column_of(tags[slot]) == spot, BLOCKED, 0.0)
+
+    half = rows // 2
+
+    def normed(index, part):
+        at = pl.ds(part * half, half)
+        xs[index, 0, at, :] = layer_norm(
+            stream[at, :].astype(f32), gain_ref[index : index + 1, :]
+        )
+
+    def exchange(index, part):
+        at = pl.ds(part * half, half)
+        send(
+            ("n", index, part), xs.at[index, 0, at], xs.at[index, 1, at],
+            pair if index else partner,
+        )
+
+    def exchanged(index, part):
+        arrive(("n", index, part), xs.at[index, 1, pl.ds(part * half, half)])
+
+    column = column_of(order_ref[...])[:, :1]
+    picks = (column == lax.broadcasted_iota(jnp.int32, (1, rows), 1).astype(f32)).astype(bf16)
+    stream[...] = jnp.dot(picks, points_ref[...], preferred_element_type=f32).astype(bf16)
+    normed(0, 0)
+    normed(0, 1)
+    tags[0] = tag_ref[...]
+    spot = (lane % HEAD_DIM).astype(f32)
+    own = column_of(tag_ref[...])
+    tag_q[...] = jnp.where((spot < SCANS) & (own != spot), 1.0, 0.0)
+    tag_k[0] = key_tags(0)
+
+    pl.semaphore_wait(barrier, 5)
+    first(0, 0)
+    send(("t", 0), tag_ref, tags.at[1], partner)
+    send(("t", 1), tag_ref, tags.at[2], pair)
+    exchange(0, 0)
+    exchange(0, 1)
+    first(0, 1)
+    first(0, 2)
+    for index in range(layers):
+        for chunk in range(3):
+            share(index, chunk)
+    for chunk in range(3):
+        first(1, chunk)
+
+    def project(index, k, side, q_at):
+        result = jnp.dot(xs[index, side], wq[index, k], preferred_element_type=f32)
+        left, middle, right = (result[:, LANES * n : LANES * (n + 1)] for n in range(3))
+        at = pl.ds(side * rows, rows)
+        marks = tag_k[side]
+        keys[0, at, :] = jnp.where(low, marks, left).astype(bf16)
+        values[0, at, :] = jnp.where(low, middle, 1.0).astype(bf16)
+        keys[1, at, :] = jnp.where(low, right, marks).astype(bf16)
+        values[1, at, :] = jnp.where(low, 1.0, right).astype(bf16)
+        if side == 0:
+            marks = tag_q[...]
+            query[q_at, 0] = jnp.where(
+                low, marks, pltpu.roll(left * LOG2_SCALE, HEAD_DIM, 1)
+            ).astype(bf16)
+            query[q_at, 1] = jnp.where(
+                low, pltpu.roll(middle * LOG2_SCALE, HEAD_DIM, 1), marks
+            ).astype(bf16)
+
+    def scores(q_at, head, at, over):
+        return lax.dot_general(
+            query[q_at, head, at, :], keys[head, over, :], (((1,), (1,)), ((), ())),
+            preferred_element_type=f32,
+        )
+
+    def settle(k, at, sums):
+        parts = [s / pltpu.roll(s, HEAD_DIM, 1) for s in sums]
+        att[k, at, :] = jnp.where(low, parts[0], parts[1]).astype(bf16)
+
+    row_blocks = [pl.ds(r * (rows // 2), rows // 2) for r in range(2)]
+
+    def attend(k):
+        for at in row_blocks:
+            sums = []
+            for head in range(2):
+                table = scores(0, head, at, slice(None))
+                top = jnp.max(table, axis=-1, keepdims=True)
+                expo = jnp.exp2(table - top).astype(bf16)
+                sums.append(jnp.dot(expo, values[head], preferred_element_type=f32))
+            settle(k, at, sums)
+
+    def attend_own(k):
+        over = pl.ds(0, rows)
+        for at in row_blocks:
+            for head in range(2):
+                table = scores(k, head, at, over)
+                top = jnp.max(table, axis=-1, keepdims=True)
+                expo = jnp.exp2(table - top).astype(bf16)
+                acc[k, head, at, :] = jnp.dot(
+                    expo, values[head, over, :], preferred_element_type=f32
+                )
+                peak[k, head, at, :] = jnp.broadcast_to(top, (rows // 2, LANES))
+
+    def attend_pair(k):
+        over = pl.ds(rows, rows)
+        for at in row_blocks:
+            sums = []
+            for head in range(2):
+                table = scores(k, head, at, over)
+                before = peak[k, head, at, :]
+                top = jnp.maximum(before[:, :1], jnp.max(table, axis=-1, keepdims=True))
+                expo = jnp.exp2(table - top).astype(bf16)
+                sums.append(
+                    jnp.dot(expo, values[head, over, :], preferred_element_type=f32)
+                    + acc[k, head, at, :] * jnp.exp2(before - top)
+                )
+            settle(k, at, sums)
+
+    def leave(index, part):
+        at = pl.ds(part * half, half)
+        result = stream[at, :].astype(f32)
+        for slot, (one, two) in enumerate(((0, 1), (2, 3), (4, 6), (5, 7))):
+            result += jnp.dot(
+                jnp.concatenate([att[one, at, :], att[two, at, :]], axis=1),
+                wo[index, slot],
+                preferred_element_type=f32,
+            )
+        return result.astype(bf16)
+
+    def run(events, body):
+        def step(k, carry):
+            for when, todo in events.items():
+                @pl.when(k == when)
+                def _(todo=todo):
+                    for event, args in todo:
+                        event(*args)
+            body(k)
+            return carry
+
+        lax.fori_loop(0, steps, step, 0)
+
+    arrive(("t", 0), tags.at[1])
+    tag_k[1] = key_tags(1)
+    exchanged(0, 0)
+    exchanged(0, 1)
+
+    def whole(k):
+        project(0, k, 0, 0)
+        project(0, k, 1, 0)
+        attend(k)
+
+    def loaded(n):
+        load(n).wait()
+
+    run(
+        {
+            0: [(loaded, (0,)), (loaded, (1,))],
+            1: [(second, (0, 0))],
+            2: [(shared, (0, 0)), (third, (0, 0))],
+            3: [(shared, (0, 1)), (second, (0, 1))],
+            4: [(fourth, (0, 0)), (third, (0, 1)), (second, (0, 2))],
+            5: [(third, (0, 2)), (fifth, (0, 0))],
+            6: [(fourth, (0, 1)), (second, (1, 0))],
+            7: [(fourth, (0, 2)), (third, (1, 0)), (fifth, (0, 1))],
+        },
+        whole,
+    )
+    loaded(2)
+    shared(0, 2)
+    fifth(0, 2)
+    for part in range(2):
+        at = pl.ds(part * half, half)
+        stream[at, :] = leave(0, part)
+        normed(1, part)
+        exchange(1, part)
+    second(1, 1)
+    arrive(("t", 1), tags.at[2])
+    tag_k[1] = key_tags(2)
+
+    def inner(k):
+        project(1, k, 0, k)
+        attend_own(k)
+
+    run(
+        {
+            0: [(loaded, (3,)), (loaded, (4,))],
+            1: [(third, (1, 1))],
+            2: [(shared, (1, 0)), (fourth, (1, 0))],
+            3: [(shared, (1, 1)), (second, (1, 2))],
+            5: [(fifth, (1, 0)), (third, (1, 2))],
+            6: [(fourth, (1, 1))],
+            7: [(fifth, (1, 1))],
+        },
+        inner,
+    )
+    fourth(1, 2)
+    exchanged(1, 0)
+    exchanged(1, 1)
+
+    def outer(k):
+        project(1, k, 1, k)
+        attend_pair(k)
+
+    run({}, outer)
+    loaded(5)
+    shared(1, 2)
+    fifth(1, 2)
+    for part in range(2):
+        out_ref[pl.ds(part * half, half), :] = leave(1, part)
+
+    for key, src, dst, device in order_of_sends:
+        copy(key, src, dst, device).wait_send()
+
+
+def fused(points, order, scan_ids, ln_gain, w_qkv, w_out):
+    rows, width = points.shape
+    peers, ranges = lax.axis_size("head"), lax.axis_size("curve")
+    layers, _, columns = w_qkv.shape
+    columns //= 2
+    steps = 2 * peers
+    vmem, far = pl.BlockSpec(memory_space=pltpu.VMEM), pl.BlockSpec(memory_space=pl.ANY)
+    dma = pltpu.SemaphoreType.DMA
+    bf16, f32 = jnp.bfloat16, jnp.float32
+    return pl.pallas_call(
+        functools.partial(fused_kernel, peers, ranges),
+        out_shape=jax.ShapeDtypeStruct((rows, width), bf16),
+        in_specs=[vmem] * 4 + [far] * 2,
+        out_specs=vmem,
+        scratch_shapes=[
+            pltpu.VMEM((layers, 2, rows, width), bf16),
+            pltpu.VMEM((rows, width), bf16),
+            pltpu.VMEM((layers, steps, width, columns), bf16),
+            pltpu.VMEM((layers, peers, width // peers, width), bf16),
+            pltpu.VMEM((steps, 2, rows, LANES), bf16),
+            pltpu.VMEM((2, 2 * rows, LANES), bf16),
+            pltpu.VMEM((2, 2 * rows, LANES), bf16),
+            pltpu.VMEM((steps, rows, LANES), bf16),
+            pltpu.VMEM((steps, 2, rows, LANES), f32),
+            pltpu.VMEM((steps, 2, rows, LANES), f32),
+            pltpu.VMEM((3, 1, rows), jnp.int32),
+            pltpu.VMEM((rows, LANES), f32),
+            pltpu.VMEM((2, rows, LANES), f32),
+            dma((96,)),
+            dma((96,)),
+            dma((3 * layers,)),
+        ],
+        compiler_params=pltpu.CompilerParams(
+            collective_id=0, has_side_effects=True, vmem_limit_bytes=60 * 1024 * 1024
+        ),
+        cost_estimate=pl.CostEstimate(
+            flops=80 * rows * width * width, bytes_accessed=20 * rows * width, transcendentals=0
+        ),
+    )(points, order, scan_ids.reshape(1, -1), ln_gain, w_qkv, w_out)
+
+
+def chip_holds_window(points, w_qkv):
+    peers, ranges = lax.axis_size("head"), lax.axis_size("curve")
+    rows, width = points.shape
+    return (
+        peers == 4
+        and ranges % 4 == 0
+        and PATCH == 2 * rows
+        and w_qkv.shape[0] == 2
+        and w_qkv.shape[2] == 12 * HEAD_DIM
+        and width == peers * 4 * HEAD_DIM
+    )
+
+
 def on_device(points, order, scan_ids, ln_gain, w_qkv, w_out):
+    if chip_holds_window(points, w_qkv):
+        return fused(points, order, scan_ids, ln_gain, w_qkv, w_out)
     stream = points[order[0]]
     tag_row = scan_ids.reshape(1, 1, -1)
     for index in range(2):

time: 152 us -> 104 us (0.68)
  Pallas kernels: 136 us -> 102 us
  other arithmetic: 7.3 us -> 0 us
  local copies, waits for them, and re-layouts: 8.11 us -> 2.26 us
    pallas_call x2 -> x1, Pallas kernels: 136 us -> 102 us  [fused(): pl.pallas_call(functools.partial(fused_kernel, peers, ranges), out_shape=...]
    reduce_sum x4 -> x0, other arithmetic: 3.79 us -> none  [the longest x2 2.06 us: layer_norm(): spread = jnp.mean(center * center, axis=-1, keepdims=True)]
    squeeze x2 -> x0, local copies, waits for them, and re-layouts: 2.95 us -> none  [on_device(): stream = layer(index, stream, normed, tag_row, w_qkv[index], w_out[index])]
    convert_element_type x2 -> x0, other arithmetic: 2.7 us -> none  [layer_norm(): return (center * lax.rsqrt(spread + EPSILON) * gain).astype(jnp.bfloat16)]
    gather x1 -> x0, local copies, waits for them, and re-layouts: 2.06 us -> none  [on_device(): stream = points[order[0]]]
where the time goes in v1:
time: 104 us
  Pallas kernels  102 us (98%)
  local copies, waits for them, and re-layouts  2.26 us (2%)
    pallas_call x1, Pallas kernels, fused(): pl.pallas_call(functools.partial(fused_kernel, peers, ranges), out_shape=...  102 us
    unnamed x1, local copies, waits for them, and re-layouts  2.26 us

profile of v1, /device:TPU:0, one launch (start us, length us, event | category | flops | bytes accessed | tf_op | source)
XLA Modules:
  0.0 104.2 jit_solution(7726478725709698870)
XLA Ops:
  0.0 102.0 %shard_map.64 = bf16[512,1024]{1,0:T(8,128)(2,1)} custom-call(bf16[512,1024]{1,0:T(8,128)(2,1)} %points_ref.1, s32[1,512]{1,0:T(1,128)} %order_ref.1, s32[1,512]{1,0:T(1,128)} %bitcast.1, f32[2,1024]{1,0:T(2,128)} %gain_ref.1, bf16[2,1024,768]{2,1,0:T(8,128)(2,1)} %wq_hbm.1, bf16[2,256,1024]{2,1,0:T(8,128)(2,1)} %wo_hbm.1), custom_call_target="tpu_custom_call" | custom-call | flops 42949672960 | bytes 10485760 | tf_op jit(solution)/shard_map/pallas_call | solution.py:702
  102.0 2.3 %copy.8 = bf16[512,1024]{1,0:T(8,128)(2,1)} copy(bf16[512,1024]{1,0:T(8,128)(2,1)} %shard_map.64) | data formatting | bytes 2097152

commit v2 on v1

--- a/solution.py
+++ b/solution.py
@@ -337,7 +337,7 @@
 
 
 def pieces(index, extent):
-    alone = extent // 8 if index == 0 else 0
+    alone = extent // 8
     return alone, (extent - 2 * alone) // 4
 
 
@@ -345,7 +345,7 @@
     peers, ranges,
     points_ref, order_ref, tag_ref, gain_ref, wq_hbm, wo_hbm, out_ref,
     xs, stream, wq, wo, query, keys, values, att, acc, peak, tags, tag_q, tag_k,
-    send_sem, recv_sem, load_sem,
+    given, send_sem, recv_sem, load_sem, given_send, given_recv,
 ):
     rows, width = points_ref.shape
     layers, steps, _, columns = wq.shape
@@ -452,6 +452,10 @@
         for c, part in enumerate(parts_of[index, chunk, "as"]):
             arrive(("y", index, chunk, "as", c), part)
             send(("x", index, chunk, "a", c), part, part, beside)
+
+    def then(index, chunk):
+        if index:
+            third(index, chunk)
         for c, part in enumerate(parts_of[index, chunk, "qos"]):
             arrive(("x", index, chunk, "q", c), part)
             send(("z", index, chunk, "o", c), part, part, above)
@@ -463,7 +467,8 @@
             arrive(("z", index, chunk, "s", c), part)
         for c, part in enumerate(parts_of[index, chunk, "qoo"]):
             arrive(("z", index, chunk, "o", c), part)
-        send(("f", index, chunk), homes[index, chunk][1], theres[index, chunk], partner)
+        if index or chunk == 2:
+            send(("f", index, chunk), homes[index, chunk][1], theres[index, chunk], partner)
 
     def fifth(index, chunk):
         arrive(("f", index, chunk), theres[index, chunk])
@@ -479,10 +484,6 @@
 
     def column_of(row):
         return jnp.transpose(jnp.broadcast_to(row.astype(f32), (LANES, row.shape[1])))
-
-    def key_tags(slot):
-        spot = (lane % HEAD_DIM).astype(f32)
-        return jnp.where(column_of(tags[slot]) == spot, BLOCKED, 0.0)
 
     half = rows // 2
 
@@ -502,97 +503,149 @@
     def exchanged(index, part):
         arrive(("n", index, part), xs.at[index, 1, pl.ds(part * half, half)])
 
+    pl.semaphore_wait(barrier, 5)
+    for chunk in range(3):
+        first(0, chunk)
     column = column_of(order_ref[...])[:, :1]
     picks = (column == lax.broadcasted_iota(jnp.int32, (1, rows), 1).astype(f32)).astype(bf16)
     stream[...] = jnp.dot(picks, points_ref[...], preferred_element_type=f32).astype(bf16)
     normed(0, 0)
     normed(0, 1)
-    tags[0] = tag_ref[...]
     spot = (lane % HEAD_DIM).astype(f32)
-    own = column_of(tag_ref[...])
-    tag_q[...] = jnp.where((spot < SCANS) & (own != spot), 1.0, 0.0)
-    tag_k[0] = key_tags(0)
-
-    pl.semaphore_wait(barrier, 5)
-    first(0, 0)
-    send(("t", 0), tag_ref, tags.at[1], partner)
-    send(("t", 1), tag_ref, tags.at[2], pair)
+
+    def mark(side, row):
+        own = column_of(row)
+        tag_q[side] = jnp.where((spot < SCANS) & (own != spot), 1.0, 0.0)
+        tag_k[side] = jnp.where(own == spot, BLOCKED, 0.0)
+
+    mark(0, tag_ref[...])
+
+    send(("t", 0), tag_ref, tags.at[0], partner)
+    send(("t", 1), tag_ref, tags.at[1], pair)
     exchange(0, 0)
     exchange(0, 1)
-    first(0, 1)
-    first(0, 2)
-    for index in range(layers):
-        for chunk in range(3):
-            share(index, chunk)
+    share(0, 2)
+    for chunk in range(3):
+        share(1, chunk)
     for chunk in range(3):
         first(1, chunk)
 
-    def project(index, k, side, q_at):
+    def place(side, turn, left, right, middle):
+        at = pl.ds(side * rows, rows)
+        marks = tag_k[side]
+        keys[turn, 0, at, :] = jnp.where(low, marks, left).astype(bf16)
+        values[turn, 0, at, :] = jnp.where(low, middle, 1.0).astype(bf16)
+        keys[turn, 1, at, :] = jnp.where(low, right, marks).astype(bf16)
+        values[turn, 1, at, :] = jnp.where(low, 1.0, right).astype(bf16)
+
+    def project(index, k, side, q_at, turn):
         result = jnp.dot(xs[index, side], wq[index, k], preferred_element_type=f32)
         left, middle, right = (result[:, LANES * n : LANES * (n + 1)] for n in range(3))
-        at = pl.ds(side * rows, rows)
-        marks = tag_k[side]
-        keys[0, at, :] = jnp.where(low, marks, left).astype(bf16)
-        values[0, at, :] = jnp.where(low, middle, 1.0).astype(bf16)
-        keys[1, at, :] = jnp.where(low, right, marks).astype(bf16)
-        values[1, at, :] = jnp.where(low, 1.0, right).astype(bf16)
-        if side == 0:
-            marks = tag_q[...]
-            query[q_at, 0] = jnp.where(
-                low, marks, pltpu.roll(left * LOG2_SCALE, HEAD_DIM, 1)
-            ).astype(bf16)
-            query[q_at, 1] = jnp.where(
-                low, pltpu.roll(middle * LOG2_SCALE, HEAD_DIM, 1), marks
-            ).astype(bf16)
-
-    def scores(q_at, head, at, over):
+        place(side, turn, left, right, middle)
+        marks = tag_q[side]
+        query[q_at, 0] = jnp.where(
+            low, marks, pltpu.roll(left * LOG2_SCALE, HEAD_DIM, 1)
+        ).astype(bf16)
+        query[q_at, 1] = jnp.where(
+            low, pltpu.roll(middle * LOG2_SCALE, HEAD_DIM, 1), marks
+        ).astype(bf16)
+
+    def project_pair(k, turn):
+        left, middle, right = (wq[1, k, :, LANES * n : LANES * (n + 1)] for n in range(3))
+        weights = jnp.concatenate([jnp.where(low, middle, left), right], axis=1)
+        result = jnp.dot(xs[1, 1], weights, preferred_element_type=f32)
+        left, right = result[:, :LANES], result[:, LANES:]
+        place(1, turn, left, right, left)
+
+    def scores(q_at, turn, head, at, over):
         return lax.dot_general(
-            query[q_at, head, at, :], keys[head, over, :], (((1,), (1,)), ((), ())),
+            query[q_at, head, at, :], keys[turn, head, over, :], (((1,), (1,)), ((), ())),
             preferred_element_type=f32,
         )
 
-    def settle(k, at, sums):
-        parts = [s / pltpu.roll(s, HEAD_DIM, 1) for s in sums]
-        att[k, at, :] = jnp.where(low, parts[0], parts[1]).astype(bf16)
-
-    row_blocks = [pl.ds(r * (rows // 2), rows // 2) for r in range(2)]
-
-    def attend(k):
+    def settle(target, k, at, sums):
+        parts = [t / pltpu.roll(t, HEAD_DIM, 1) for t in sums]
+        target[k, at, :] = jnp.where(low, parts[0], parts[1]).astype(bf16)
+
+    row_blocks = [pl.ds(r * half, half) for r in range(2)]
+
+    def flow(units, beside_first=None):
+        table = units[0][0]()
+        for n, (_, use) in enumerate(units):
+            ahead = units[n + 1][0]() if n + 1 < len(units) else None
+            if n == 0 and beside_first is not None:
+                beside_first()
+            use(table)
+            table = ahead
+
+    def attend(side, finish):
+        units = []
         for at in row_blocks:
             sums = []
             for head in range(2):
-                table = scores(0, head, at, slice(None))
-                top = jnp.max(table, axis=-1, keepdims=True)
-                expo = jnp.exp2(table - top).astype(bf16)
-                sums.append(jnp.dot(expo, values[head], preferred_element_type=f32))
-            settle(k, at, sums)
-
-    def attend_own(k):
+                def look(head=head, at=at):
+                    return scores(side, 0, head, at, slice(None))
+
+                def use(table, head=head, at=at, sums=sums):
+                    top = jnp.max(table, axis=-1, keepdims=True)
+                    expo = jnp.exp2(table - top).astype(bf16)
+                    sums.append(
+                        jnp.dot(expo, values[0, head], preferred_element_type=f32)
+                    )
+                    if head == 1:
+                        finish(at, sums)
+
+                units.append((look, use))
+        return units
+
+    def attend_own(k, turn):
         over = pl.ds(0, rows)
+        units = []
         for at in row_blocks:
             for head in range(2):
-                table = scores(k, head, at, over)
-                top = jnp.max(table, axis=-1, keepdims=True)
-                expo = jnp.exp2(table - top).astype(bf16)
-                acc[k, head, at, :] = jnp.dot(
-                    expo, values[head, over, :], preferred_element_type=f32
-                )
-                peak[k, head, at, :] = jnp.broadcast_to(top, (rows // 2, LANES))
-
-    def attend_pair(k):
+                def look(head=head, at=at):
+                    return scores(k, turn, head, at, over)
+
+                def use(table, head=head, at=at):
+                    top = jnp.max(table, axis=-1, keepdims=True)
+                    expo = jnp.exp2(table - top).astype(bf16)
+                    acc[k, head, at, :] = jnp.dot(
+                        expo, values[turn, head, over, :], preferred_element_type=f32
+                    )
+                    peak[k, head, at, :] = jnp.broadcast_to(top, (half, LANES))
+
+                units.append((look, use))
+        return units
+
+    def attend_pair(k, turn):
         over = pl.ds(rows, rows)
+        units = []
         for at in row_blocks:
             sums = []
             for head in range(2):
-                table = scores(k, head, at, over)
-                before = peak[k, head, at, :]
-                top = jnp.maximum(before[:, :1], jnp.max(table, axis=-1, keepdims=True))
-                expo = jnp.exp2(table - top).astype(bf16)
-                sums.append(
-                    jnp.dot(expo, values[head, over, :], preferred_element_type=f32)
-                    + acc[k, head, at, :] * jnp.exp2(before - top)
-                )
-            settle(k, at, sums)
+                def look(head=head, at=at):
+                    return scores(k, turn, head, at, over)
+
+                def use(table, head=head, at=at, sums=sums):
+                    before = peak[k, head, at, :]
+                    highest = jnp.max(table, axis=-1, keepdims=True)
+                    top = jnp.maximum(before, jnp.broadcast_to(highest, (half, LANES)))
+                    expo = jnp.concatenate(
+                        [
+                            jnp.exp2(table[:, LANES * n : LANES * (n + 1)] - top).astype(bf16)
+                            for n in range(rows // LANES)
+                        ],
+                        axis=1,
+                    )
+                    sums.append(
+                        jnp.dot(expo, values[turn, head, over, :], preferred_element_type=f32)
+                        + acc[k, head, at, :] * jnp.exp2(before - top)
+                    )
+                    if head == 1:
+                        settle(att, k, at, sums)
+
+                units.append((look, use))
+        return units
 
     def leave(index, part):
         at = pl.ds(part * half, half)
@@ -605,81 +658,118 @@
             )
         return result.astype(bf16)
 
-    def run(events, body):
+    def run(count, events, *phases):
         def step(k, carry):
-            for when, todo in events.items():
-                @pl.when(k == when)
-                def _(todo=todo):
-                    for event, args in todo:
-                        event(*args)
-            body(k)
+            for n, phase in enumerate(phases):
+                for (when, place_in), todo in events.items():
+                    if place_in == n:
+
+                        @pl.when(k == when)
+                        def _(todo=todo):
+                            for event, args in todo:
+                                event(*args)
+
+                phase(k)
             return carry
 
-        lax.fori_loop(0, steps, step, 0)
-
-    arrive(("t", 0), tags.at[1])
-    tag_k[1] = key_tags(1)
+        lax.fori_loop(0, count, step, 0)
+
+    arrive(("t", 0), tags.at[0])
+    mark(1, tags[0])
     exchanged(0, 0)
     exchanged(0, 1)
 
-    def whole(k):
-        project(0, k, 0, 0)
-        project(0, k, 1, 0)
-        attend(k)
-
     def loaded(n):
         load(n).wait()
 
+    def slot_of(k):
+        return k + k // 2 * k
+
+    def handed(k):
+        to = 2 + k + k // 2 * (k - 1)
+        return remote(given.at[k], att.at[to], given_send.at[k], given_recv.at[k], partner)
+
+    def taken(k):
+        to = 2 + k + k // 2 * (k - 1)
+        part = att.at[to]
+        return remote(part, part, given_send.at[k], given_recv.at[k], partner)
+
+    def make(k):
+        slot = slot_of(k)
+        for side in range(2):
+            project(0, slot, side, side, 0)
+
+    def weigh(k):
+        def give(at, sums):
+            settle(given, k, at, sums)
+            if at is row_blocks[-1]:
+                handed(k).start()
+
+        def keep(at, sums):
+            settle(att, slot_of(k), at, sums)
+
+        flow(attend(1, give) + attend(0, keep))
+
     run(
+        4,
         {
-            0: [(loaded, (0,)), (loaded, (1,))],
-            1: [(second, (0, 0))],
-            2: [(shared, (0, 0)), (third, (0, 0))],
-            3: [(shared, (0, 1)), (second, (0, 1))],
-            4: [(fourth, (0, 0)), (third, (0, 1)), (second, (0, 2))],
-            5: [(third, (0, 2)), (fifth, (0, 0))],
-            6: [(fourth, (0, 1)), (second, (1, 0))],
-            7: [(fourth, (0, 2)), (third, (1, 0)), (fifth, (0, 1))],
+            (0, 0): [(loaded, (0,)), (loaded, (1,))],
+            (0, 1): [(second, (0, 0))],
+            (1, 0): [(third, (0, 0)), (then, (0, 0))],
+            (1, 1): [(second, (0, 1)), (third, (0, 1))],
+            (2, 0): [(then, (0, 1)), (fourth, (0, 0))],
+            (2, 1): [(second, (0, 2)), (third, (0, 2))],
+            (3, 0): [(then, (0, 2)), (fourth, (0, 1)), (second, (1, 0))],
+            (3, 1): [(fourth, (0, 2))],
         },
-        whole,
+        make, weigh,
     )
+    then(1, 0)
+    second(1, 1)
     loaded(2)
     shared(0, 2)
     fifth(0, 2)
+    for k in range(4):
+        taken(k).wait_recv()
     for part in range(2):
         at = pl.ds(part * half, half)
         stream[at, :] = leave(0, part)
         normed(1, part)
         exchange(1, part)
-    second(1, 1)
-    arrive(("t", 1), tags.at[2])
-    tag_k[1] = key_tags(2)
+    then(1, 1)
+    second(1, 2)
+    arrive(("t", 1), tags.at[1])
+    mark(1, tags[1])
+
+    loaded(3)
+    loaded(4)
+    project(1, 0, 0, 0, 0)
 
     def inner(k):
-        project(1, k, 0, k)
-        attend_own(k)
+        flow(attend_own(k, k % 2), lambda: project(1, k + 1, 0, k + 1, (k + 1) % 2))
 
     run(
+        steps - 1,
         {
-            0: [(loaded, (3,)), (loaded, (4,))],
-            1: [(third, (1, 1))],
-            2: [(shared, (1, 0)), (fourth, (1, 0))],
-            3: [(shared, (1, 1)), (second, (1, 2))],
-            5: [(fifth, (1, 0)), (third, (1, 2))],
-            6: [(fourth, (1, 1))],
-            7: [(fifth, (1, 1))],
+            (1, 0): [(shared, (1, 0)), (fourth, (1, 0)), (then, (1, 2))],
+            (2, 0): [(shared, (1, 1))],
+            (3, 0): [],
+            (4, 0): [(fifth, (1, 0)), (fourth, (1, 1))],
+            (6, 0): [(fourth, (1, 2)), (fifth, (1, 1))],
         },
         inner,
     )
-    fourth(1, 2)
+    flow(attend_own(steps - 1, 1))
     exchanged(1, 0)
     exchanged(1, 1)
 
+    project_pair(0, 0)
+
     def outer(k):
-        project(1, k, 1, k)
-        attend_pair(k)
-
-    run({}, outer)
+        flow(attend_pair(k, k % 2), lambda: project_pair(k + 1, (k + 1) % 2))
+
+    run(steps - 1, {}, outer)
+    flow(attend_pair(steps - 1, 1))
     loaded(5)
     shared(1, 2)
     fifth(1, 2)
@@ -688,6 +778,8 @@
 
     for key, src, dst, device in order_of_sends:
         copy(key, src, dst, device).wait_send()
+    for k in range(4):
+        handed(k).wait_send()
 
 
 def fused(points, order, scan_ids, ln_gain, w_qkv, w_out):
@@ -710,17 +802,20 @@
             pltpu.VMEM((layers, steps, width, columns), bf16),
             pltpu.VMEM((layers, peers, width // peers, width), bf16),
             pltpu.VMEM((steps, 2, rows, LANES), bf16),
-            pltpu.VMEM((2, 2 * rows, LANES), bf16),
-            pltpu.VMEM((2, 2 * rows, LANES), bf16),
+            pltpu.VMEM((2, 2, 2 * rows, LANES), bf16),
+            pltpu.VMEM((2, 2, 2 * rows, LANES), bf16),
             pltpu.VMEM((steps, rows, LANES), bf16),
             pltpu.VMEM((steps, 2, rows, LANES), f32),
             pltpu.VMEM((steps, 2, rows, LANES), f32),
-            pltpu.VMEM((3, 1, rows), jnp.int32),
-            pltpu.VMEM((rows, LANES), f32),
+            pltpu.VMEM((2, 1, rows), jnp.int32),
             pltpu.VMEM((2, rows, LANES), f32),
+            pltpu.VMEM((2, rows, LANES), f32),
+            pltpu.VMEM((steps // 2, rows, LANES), bf16),
             dma((96,)),
             dma((96,)),
             dma((3 * layers,)),
+            dma((steps // 2,)),
+            dma((steps // 2,)),
         ],
         compiler_params=pltpu.CompilerParams(
             collective_id=0, has_side_effects=True, vmem_limit_bytes=60 * 1024 * 1024

time: 104 us -> 87.8 us (0.84)
  Pallas kernels: 102 us -> 85.3 us
    pallas_call x1, Pallas kernels: 102 us -> 85.3 us  [fused(): pl.pallas_call(functools.partial(fused_kernel, peers, ranges), out_shape=...]
where the time goes in v2:
time: 87.8 us; the launch traced here: 87.6 us
  Pallas kernels  85.3 us (97%)
  local copies, waits for them, and re-layouts  2.26 us (3%)
    pallas_call x1, Pallas kernels, fused(): pl.pallas_call(functools.partial(fused_kernel, peers, ranges), out_shape=...  85.3 us
    unnamed x1, local copies, waits for them, and re-layouts  2.26 us

profile of v2, /device:TPU:0, one launch (start us, length us, event | category | flops | bytes accessed | tf_op | source)
XLA Modules:
  0.0 87.6 jit_solution(2852328379048783483)
XLA Ops:
  0.0 85.3 %shard_map.64 = bf16[512,1024]{1,0:T(8,128)(2,1)} custom-call(bf16[512,1024]{1,0:T(8,128)(2,1)} %points_ref.1, s32[1,512]{1,0:T(1,128)} %order_ref.1, s32[1,512]{1,0:T(1,128)} %bitcast.1, f32[2,1024]{1,0:T(2,128)} %gain_ref.1, bf16[2,1024,768]{2,1,0:T(8,128)(2,1)} %wq_hbm.1, bf16[2,256,1024]{2,1,0:T(8,128)(2,1)} %wo_hbm.1), custom_call_target="tpu_custom_call" | custom-call | flops 42949672960 | bytes 10485760 | tf_op jit(solution)/shard_map/pallas_call | solution.py:794
  85.3 2.3 %copy.8 = bf16[512,1024]{1,0:T(8,128)(2,1)} copy(bf16[512,1024]{1,0:T(8,128)(2,1)} %shard_map.64) | data formatting | bytes 2097152

commit v3 on v2

--- a/solution.py
+++ b/solution.py
@@ -751,17 +751,18 @@
     run(
         steps - 1,
         {
-            (1, 0): [(shared, (1, 0)), (fourth, (1, 0)), (then, (1, 2))],
+            (1, 0): [(shared, (1, 0)), (fourth, (1, 0))],
             (2, 0): [(shared, (1, 1))],
             (3, 0): [],
             (4, 0): [(fifth, (1, 0)), (fourth, (1, 1))],
-            (6, 0): [(fourth, (1, 2)), (fifth, (1, 1))],
+            (6, 0): [(then, (1, 2)), (fifth, (1, 1))],
         },
         inner,
     )
     flow(attend_own(steps - 1, 1))
     exchanged(1, 0)
     exchanged(1, 1)
+    fourth(1, 2)
 
     project_pair(0, 0)
 

time: 87.8 us -> 86.9 us (0.990); the launches traced: 87.6 us -> 85.3 us
  Pallas kernels: 85.3 us -> 83 us
    pallas_call x1, Pallas kernels: 85.3 us -> 83 us  [fused(): pl.pallas_call(functools.partial(fused_kernel, peers, ranges), out_shape=...]
where the time goes in v3:
time: 86.9 us; the launch traced here: 85.3 us
  Pallas kernels  83 us (96%)
  local copies, waits for them, and re-layouts  2.26 us (3%)
    pallas_call x1, Pallas kernels, fused(): pl.pallas_call(functools.partial(fused_kernel, peers, ranges), out_shape=...  83 us
    unnamed x1, local copies, waits for them, and re-layouts  2.26 us

profile of v3, /device:TPU:0, one launch (start us, length us, event | category | flops | bytes accessed | tf_op | source)
XLA Modules:
  0.0 85.3 jit_solution(887775535379807400)
XLA Ops:
  0.0 83.0 %shard_map.64 = bf16[512,1024]{1,0:T(8,128)(2,1)} custom-call(bf16[512,1024]{1,0:T(8,128)(2,1)} %points_ref.1, s32[1,512]{1,0:T(1,128)} %order_ref.1, s32[1,512]{1,0:T(1,128)} %bitcast.1, f32[2,1024]{1,0:T(2,128)} %gain_ref.1, bf16[2,1024,768]{2,1,0:T(8,128)(2,1)} %wq_hbm.1, bf16[2,256,1024]{2,1,0:T(8,128)(2,1)} %wo_hbm.1), custom_call_target="tpu_custom_call" | custom-call | flops 42949672960 | bytes 10485760 | tf_op jit(solution)/shard_map/pallas_call | solution.py:795
  83.0 2.3 %copy.8 = bf16[512,1024]{1,0:T(8,128)(2,1)} copy(bf16[512,1024]{1,0:T(8,128)(2,1)} %shard_map.64) | data formatting | bytes 2097152

commit v4 on v3

--- a/solution.py
+++ b/solution.py
@@ -509,8 +509,9 @@
     column = column_of(order_ref[...])[:, :1]
     picks = (column == lax.broadcasted_iota(jnp.int32, (1, rows), 1).astype(f32)).astype(bf16)
     stream[...] = jnp.dot(picks, points_ref[...], preferred_element_type=f32).astype(bf16)
-    normed(0, 0)
-    normed(0, 1)
+    for part in range(2):
+        normed(0, part)
+        exchange(0, part)
     spot = (lane % HEAD_DIM).astype(f32)
 
     def mark(side, row):
@@ -522,8 +523,6 @@
 
     send(("t", 0), tag_ref, tags.at[0], partner)
     send(("t", 1), tag_ref, tags.at[1], pair)
-    exchange(0, 0)
-    exchange(0, 1)
     share(0, 2)
     for chunk in range(3):
         share(1, chunk)

time: 86.9 us -> 86.8 us (level)
  no operation moved by 1% of the time
where the time goes in v4:
time: 86.8 us; the launch traced here: 85.4 us
  Pallas kernels  83.1 us (96%)
  local copies, waits for them, and re-layouts  2.26 us (3%)
    pallas_call x1, Pallas kernels, fused(): pl.pallas_call(functools.partial(fused_kernel, peers, ranges), out_shape=...  83.1 us
    unnamed x1, local copies, waits for them, and re-layouts  2.26 us

profile of v4, /device:TPU:0, one launch (start us, length us, event | category | flops | bytes accessed | tf_op | source)
XLA Modules:
  0.0 85.4 jit_solution(6862810291029010221)
XLA Ops:
  0.0 83.1 %shard_map.64 = bf16[512,1024]{1,0:T(8,128)(2,1)} custom-call(bf16[512,1024]{1,0:T(8,128)(2,1)} %points_ref.1, s32[1,512]{1,0:T(1,128)} %order_ref.1, s32[1,512]{1,0:T(1,128)} %bitcast.1, f32[2,1024]{1,0:T(2,128)} %gain_ref.1, bf16[2,1024,768]{2,1,0:T(8,128)(2,1)} %wq_hbm.1, bf16[2,256,1024]{2,1,0:T(8,128)(2,1)} %wo_hbm.1), custom_call_target="tpu_custom_call" | custom-call | flops 42949672960 | bytes 10485760 | tf_op jit(solution)/shard_map/pallas_call | solution.py:794
  83.1 2.3 %copy.8 = bf16[512,1024]{1,0:T(8,128)(2,1)} copy(bf16[512,1024]{1,0:T(8,128)(2,1)} %shard_map.64) | data formatting | bytes 2097152
